TPU v7x, 32 devices: a whole 2x2x4 slice. The times are simulated.
32 devices in a mesh: batch: 16 (over z, y, x), cols: 2 (over core).
Axes of the slice: x: 2, y: 2, z: 4, core: 2. Of those that a mesh axis runs over, the one named last changes fastest.
Arguments:
- grad_up: float32 [16, 1024, 4096], P('batch', None, 'cols'), may hold values from -0.875 to 0.875
- grad_down: float32 [16, 4096, 1024], P('batch', 'cols'), may hold values from -0.875 to 0.875
- grad_query: float32 [16, 1024, 1024], P('batch', None, 'cols'), may hold values from -0.875 to 0.875
- grad_key: float32 [16, 1024, 1024], P('batch', None, 'cols'), may hold values from -0.875 to 0.875
- grad_value: float32 [16, 1024, 1024], P('batch', None, 'cols'), may hold values from -0.875 to 0.875
- grad_mixed: float32 [16, 1024, 1024], P('batch', 'cols'), may hold values from -0.875 to 0.875
- grad_norm: float32 [16, 1024], P('batch'), may hold values from -8 to 8
- weight_up: float32 [1024, 4096], P('batch', 'cols'), may hold values from -0.1875 to 0.1875
- weight_down: float32 [4096, 1024], P('cols', 'batch'), may hold values from -0.09375 to 0.09375
- weight_query: float32 [1024, 1024], P('batch', 'cols'), may hold values from -0.1875 to 0.1875
- weight_key: float32 [1024, 1024], P('batch', 'cols'), may hold values from -0.1875 to 0.1875
- weight_value: float32 [1024, 1024], P('batch', 'cols'), may hold values from -0.1875 to 0.1875
- weight_mixed: float32 [1024, 1024], P('cols', 'batch'), may hold values from -0.1875 to 0.1875
- weight_norm: float32 [1024], P('batch'), may hold values from 0.25 to 1.75
Outputs:
- copy_up: bfloat16 [1024, 4096], P(None, 'cols')
- copy_down: bfloat16 [4096, 1024], P('cols')
- copy_query: bfloat16 [1024, 1024], P(None, 'cols')
- copy_key: bfloat16 [1024, 1024], P(None, 'cols')
- copy_value: bfloat16 [1024, 1024], P(None, 'cols')
- copy_mixed: bfloat16 [1024, 1024], P('cols')
- copy_norm: bfloat16 [1024], replicated
- new_up: float32 [1024, 4096], P('batch', 'cols')
- new_down: float32 [4096, 1024], P('cols', 'batch')
- new_query: float32 [1024, 1024], P('batch', 'cols')
- new_key: float32 [1024, 1024], P('batch', 'cols')
- new_value: float32 [1024, 1024], P('batch', 'cols')
- new_mixed: float32 [1024, 1024], P('cols', 'batch')
- new_norm: float32 [1024], P('batch')
All inputs are finite; a program needn't handle non-finite values.
Results may differ from a plain program's by a relative error of at most 0.0004.
Values may be sent and summed in bfloat16 or wider, within the bound.
A program may use at most 128 MiB of HBM per device.

v0:
```python
import jax
import jax.numpy as jnp
from jax import lax
from jax.sharding import PartitionSpec as P

learn_rate = 0.3


def shards(
    grad_up,
    grad_down,
    grad_query,
    grad_key,
    grad_value,
    grad_mixed,
    grad_norm,
    weight_up,
    weight_down,
    weight_query,
    weight_key,
    weight_value,
    weight_mixed,
    weight_norm,
):
    mean_up, mean_down, mean_query, mean_key, mean_value, mean_mixed, mean_norm = (
        lax.psum_scatter(grad_up[0], "batch", scatter_dimension=0, tiled=True),
        lax.psum_scatter(grad_down[0], "batch", scatter_dimension=1, tiled=True),
        lax.psum_scatter(grad_query[0], "batch", scatter_dimension=0, tiled=True),
        lax.psum_scatter(grad_key[0], "batch", scatter_dimension=0, tiled=True),
        lax.psum_scatter(grad_value[0], "batch", scatter_dimension=0, tiled=True),
        lax.psum_scatter(grad_mixed[0], "batch", scatter_dimension=1, tiled=True),
        lax.psum_scatter(grad_norm[0], "batch", scatter_dimension=0, tiled=True),
    )
    mean_rate = lax.axis_size("batch") ** (-0.5)
    mean_up = mean_up * mean_rate
    mean_down = mean_down * mean_rate
    mean_query = mean_query * mean_rate
    mean_key = mean_key * mean_rate
    mean_value = mean_value * mean_rate
    mean_mixed = mean_mixed * mean_rate
    mean_norm = mean_norm * mean_rate
    new_up = weight_up - learn_rate * mean_up
    new_down = weight_down - learn_rate * mean_down
    new_query = weight_query - learn_rate * mean_query
    new_key = weight_key - learn_rate * mean_key
    new_value = weight_value - learn_rate * mean_value
    new_mixed = weight_mixed - learn_rate * mean_mixed
    new_norm = weight_norm - learn_rate * mean_norm
    copy_up, copy_down, copy_query, copy_key, copy_value, copy_mixed, copy_norm = (
        lax.all_gather(new_up.astype(jnp.bfloat16), "batch", axis=0, tiled=True),
        lax.all_gather(new_down.astype(jnp.bfloat16), "batch", axis=1, tiled=True),
        lax.all_gather(new_query.astype(jnp.bfloat16), "batch", axis=0, tiled=True),
        lax.all_gather(new_key.astype(jnp.bfloat16), "batch", axis=0, tiled=True),
        lax.all_gather(new_value.astype(jnp.bfloat16), "batch", axis=0, tiled=True),
        lax.all_gather(new_mixed.astype(jnp.bfloat16), "batch", axis=1, tiled=True),
        lax.all_gather(new_norm.astype(jnp.bfloat16), "batch", axis=0, tiled=True),
    )
    return (
        copy_up,
        copy_down,
        copy_query,
        copy_key,
        copy_value,
        copy_mixed,
        copy_norm,
        new_up,
        new_down,
        new_query,
        new_key,
        new_value,
        new_mixed,
        new_norm,
    )


def solution(mesh):
    placed = (
        P("batch", None, "cols"),
        P("batch", "cols", None),
        P("batch", None, "cols"),
        P("batch", None, "cols"),
        P("batch", None, "cols"),
        P("batch", "cols", None),
        P("batch", None),
        P("batch", "cols"),
        P("cols", "batch"),
        P("batch", "cols"),
        P("batch", "cols"),
        P("batch", "cols"),
        P("cols", "batch"),
        P("batch"),
    )
    return jax.shard_map(
        shards,
        mesh=mesh,
        in_specs=placed,
        out_specs=(
            P(None, "cols"),
            P("cols", None),
            P(None, "cols"),
            P(None, "cols"),
            P(None, "cols"),
            P("cols", None),
            P(),
            P("batch", "cols"),
            P("cols", "batch"),
            P("batch", "cols"),
            P("batch", "cols"),
            P("batch", "cols"),
            P("cols", "batch"),
            P("batch"),
        ),
        check_vma=False,
    )
```

profile of v0, /device:TPU:0, one launch (start us, length us, event | category | flops | bytes accessed | tf_op | source)
XLA Modules:
  0.0 1104.0 jit_solution(16749740426630674211)
XLA Ops:
  7.2 0.0 reduce-scatter.11.cloned.1.call-start
  7.2 0.7 reduce-scatter.11.cloned.1.call-update
  7.9 0.0 reduce-scatter.13.cloned.1.call-start
  8.0 0.7 reduce-scatter.13.cloned.1.call-update
  8.7 0.0 reduce-scatter.15.cloned.1.call-start
  8.7 0.7 reduce-scatter.15.cloned.1.call-update
  9.4 0.0 reduce-scatter.17.cloned.1.call-start
  9.5 1.8 copy.33
  11.3 0.0 reduce-scatter.17.cloned.1.call-update
  11.3 0.0 reduce-scatter.7.cloned.1.call-start
  11.4 0.5 reduce-scatter.7.cloned.1.call-update
  11.9 0.0 reduce-scatter.9.cloned.1.call-start
  11.9 9.2 copy.32
  21.2 0.0 reduce-scatter.9.cloned.1.call-update
  21.3 0.0 all-gather.11.cloned.1.call-start
  21.3 73.1 %reduce-scatter.11.cloned.1.call-done = f32[64,512]{1,0:T(8,128)} async-done(((f32[1024,512]{1,0:T(8,128)}), f32[64,512]{1,0:T(8,128)}) %reduce-scatter.11.cloned.1.call-update) | async-done | bytes 131088 | tf_op jit(solution)/shard_map/reduce_scatter | solution.py:28
  94.5 1.6 fusion.6
  96.1 0.0 all-gather.13.cloned.1.call-start
  96.1 78.7 %reduce-scatter.13.cloned.1.call-done = f32[64,512]{1,0:T(8,128)} async-done(((f32[1024,512]{1,0:T(8,128)}), f32[64,512]{1,0:T(8,128)}) %reduce-scatter.13.cloned.1.call-update) | async-done | bytes 131088 | tf_op jit(solution)/shard_map/reduce_scatter | solution.py:29
  174.8 1.6 fusion.5
  176.4 0.0 all-gather.15.cloned.1.call-start
  176.5 78.7 %reduce-scatter.15.cloned.1.call-done = f32[64,512]{1,0:T(8,128)} async-done(((f32[1024,512]{1,0:T(8,128)}), f32[64,512]{1,0:T(8,128)}) %reduce-scatter.15.cloned.1.call-update) | async-done | bytes 131088 | tf_op jit(solution)/shard_map/reduce_scatter | solution.py:30
  255.2 1.6 fusion.4
  256.8 0.0 all-gather.17.cloned.1.call-start
  256.8 79.2 %reduce-scatter.17.cloned.1.call-done = f32[512,64]{0,1:T(8,128)} async-done(((f32[512,1024]{0,1:T(8,128)}), f32[512,64]{0,1:T(8,128)}) %reduce-scatter.17.cloned.1.call-update) | async-done | bytes 131088 | tf_op jit(solution)/shard_map/reduce_scatter | solution.py:31
  336.0 1.6 fusion.3
  337.6 0.0 all-gather.7.cloned.1.call-start
  337.7 174.8 %reduce-scatter.7.cloned.1.call-done = f32[64,2048]{1,0:T(8,128)} async-done(((f32[1024,2048]{1,0:T(8,128)}), f32[64,2048]{1,0:T(8,128)}) %reduce-scatter.7.cloned.1.call-update) | async-done | bytes 524304 | tf_op jit(solution)/shard_map/reduce_scatter | solution.py:26
  512.5 2.0 fusion.8
  514.5 0.0 all-gather.9.cloned.1.call-start
  514.5 180.4 %reduce-scatter.9.cloned.1.call-done = f32[2048,64]{0,1:T(8,128)} async-done(((f32[2048,1024]{0,1:T(8,128)}), f32[2048,64]{0,1:T(8,128)}) %reduce-scatter.9.cloned.1.call-update) | async-done | bytes 524304 | tf_op jit(solution)/shard_map/reduce_scatter | solution.py:27
  695.0 2.0 fusion.7
  697.0 0.6 fusion.9
  698.9 42.5 %all-reduce.1 = f32[1024]{0:T(1024)S(1)} all-reduce(f32[1024]{0:T(1024)S(1)} %bitcast.15), channel_id=8, replica_groups=mesh['batch'=16,'cols'=2] {'batch'}, use_global_device_ids=true, to_apply=%region_6.0.clone | all-reduce | flops 1024 | bytes 8192
  741.4 0.6 fusion.1
  742.0 0.2 dynamic-update-slice
  742.2 37.3 %all-reduce = bf16[1024]{0:T(1024)(128)(2,1)} all-reduce(bf16[1024]{0:T(1024)(128)(2,1)S(1)} %dynamic-update-slice), channel_id=1, replica_groups=mesh['batch'=16,'cols'=2] {'batch'}, use_global_device_ids=true, to_apply=%add | all-reduce | flops 1024 | bytes 4096
  779.5 33.8 %all-gather.13.cloned.1.call-done = bf16[1024,512]{1,0:T(8,128)(2,1)} async-done(((bf16[64,512]{1,0:T(8,128)(2,1)}), bf16[1024,512]{1,0:T(8,128)(2,1)}) %all-gather.13.cloned.1.call-update) | async-done | bytes 1048592 | tf_op jit(solution)/shard_map/all_gather | solution.py:53
  813.3 57.3 %all-gather.15.cloned.1.call-done = bf16[1024,512]{1,0:T(8,128)(2,1)} async-done(((bf16[64,512]{1,0:T(8,128)(2,1)}), bf16[1024,512]{1,0:T(8,128)(2,1)}) %all-gather.15.cloned.1.call-update) | async-done | bytes 1048592 | tf_op jit(solution)/shard_map/all_gather | solution.py:54
  870.6 57.1 %all-gather.17.cloned.1.call-done = bf16[512,1024]{0,1:T(8,128)(2,1)} async-done(((bf16[512,64]{0,1:T(8,128)(2,1)}), bf16[512,1024]{0,1:T(8,128)(2,1)}) %all-gather.17.cloned.1.call-update) | async-done | bytes 1048592 | tf_op jit(solution)/shard_map/all_gather | solution.py:55
  927.7 2.3 copy.35
  930.0 75.5 %all-gather.7.cloned.1.call-done = bf16[1024,2048]{1,0:T(8,128)(2,1)} async-done(((bf16[64,2048]{1,0:T(8,128)(2,1)}), bf16[1024,2048]{1,0:T(8,128)(2,1)}) %all-gather.7.cloned.1.call-update) | async-done | bytes 4194320 | tf_op jit(solution)/shard_map/all_gather | solution.py:50
  1005.5 77.4 %all-gather.9.cloned.1.call-done = bf16[2048,1024]{0,1:T(8,128)(2,1)} async-done(((bf16[2048,64]{0,1:T(8,128)(2,1)}), bf16[2048,1024]{0,1:T(8,128)(2,1)}) %all-gather.9.cloned.1.call-update) | async-done | bytes 4194320 | tf_op jit(solution)/shard_map/all_gather | solution.py:51
  1082.9 6.4 copy.34
  1089.3 4.9 copy.41
  1094.3 1.0 copy.42
  1095.3 1.0 copy.43
  1096.2 1.0 copy.44
  (34 shorter events, 0.2 us)
Async XLA Ops:
  7.2 2.3 copy-start
  7.2 87.3 %reduce-scatter.11.cloned.1.call-start = ((), (), s32[]{:S(2)}) async-start(), calls=%async_computation.10 | async-start | bytes 2228224 | tf_op jit(solution)/shard_map/reduce_scatter | solution.py:28
  7.9 166.9 %reduce-scatter.13.cloned.1.call-start = ((), (), s32[]{:S(2)}) async-start(), calls=%async_computation.12 | async-start | bytes 2228224 | tf_op jit(solution)/shard_map/reduce_scatter | solution.py:29
  8.7 246.5 %reduce-scatter.15.cloned.1.call-start = ((), (), s32[]{:S(2)}) async-start(), calls=%async_computation.14 | async-start | bytes 2228224 | tf_op jit(solution)/shard_map/reduce_scatter | solution.py:30
  9.4 326.6 %reduce-scatter.17.cloned.1.call-start = ((), (), s32[]{:S(2)}) async-start(), calls=%async_computation.16 | async-start | bytes 2228224 | tf_op jit(solution)/shard_map/reduce_scatter | solution.py:31
  11.3 501.2 %reduce-scatter.7.cloned.1.call-start = ((), (), s32[]{:S(2)}) async-start(), calls=%async_computation.6 | async-start | bytes 8912896 | tf_op jit(solution)/shard_map/reduce_scatter | solution.py:26
  11.9 683.1 %reduce-scatter.9.cloned.1.call-start = ((), (), s32[]{:S(2)}) async-start(), calls=%async_computation.8 | async-start | bytes 8912896 | tf_op jit(solution)/shard_map/reduce_scatter | solution.py:27
  21.2 73.3 %copy-start.6 = (f32[64,512]{1,0:T(8,128)S(1)}, f32[64,512]{1,0:T(8,128)}, u32[]{:S(2)}) copy-start(f32[64,512]{1,0:T(8,128)} %param.23) | copy-start | bytes 393220
  21.2 153.6 %copy-start.7 = (f32[64,512]{1,0:T(8,128)S(1)}, f32[64,512]{1,0:T(8,128)}, u32[]{:S(2)}) copy-start(f32[64,512]{1,0:T(8,128)} %param.24) | copy-start | bytes 393220
  21.2 234.0 %copy-start.8 = (f32[64,512]{1,0:T(8,128)S(1)}, f32[64,512]{1,0:T(8,128)}, u32[]{:S(2)}) copy-start(f32[64,512]{1,0:T(8,128)} %param.25) | copy-start | bytes 393220
  21.2 314.8 %copy-start.9 = (f32[512,64]{0,1:T(8,128)S(1)}, f32[512,64]{0,1:T(8,128)}, u32[]{:S(2)}) copy-start(f32[512,64]{0,1:T(8,128)} %param.26) | copy-start | bytes 393220
  21.2 491.3 %copy-start.4 = (f32[64,2048]{1,0:T(8,128)S(1)}, f32[64,2048]{1,0:T(8,128)}, u32[]{:S(2)}) copy-start(f32[64,2048]{1,0:T(8,128)} %param.21) | copy-start | bytes 1572868
  21.2 673.8 %copy-start.5 = (f32[2048,64]{0,1:T(8,128)S(1)}, f32[2048,64]{0,1:T(8,128)}, u32[]{:S(2)}) copy-start(f32[2048,64]{0,1:T(8,128)} %param.22) | copy-start | bytes 1572868
  21.2 675.8 %copy-start.11 = (u32[32]{0:T(128)S(1)}, u32[32]{0:T(128)}, u32[]{:S(2)}) copy-start(u32[32]{0:T(128)} %constant.27) | copy-start | bytes 388
  21.2 677.7 %copy-start.10 = (f32[1,1024]{1,0:T(1,128)S(1)}, f32[1,1024]{1,0:T(1,128)}, u32[]{:S(2)}) copy-start(f32[1,1024]{1,0:T(1,128)} %param.20) | copy-start | bytes 12292
  21.3 720.1 %copy-start.12 = (f32[64]{0:T(128)S(1)}, f32[64]{0:T(128)}, u32[]{:S(2)}) copy-start(f32[64]{0:T(128)} %param.27) | copy-start | bytes 772
  21.3 758.2 %all-gather.11.cloned.1.call-start = ((), (), s32[]{:S(2)}) async-start(), calls=%async_computation.11 | async-start | bytes 1114112 | tf_op jit(solution)/shard_map/all_gather | solution.py:52
  96.1 717.2 %all-gather.13.cloned.1.call-start = ((), (), s32[]{:S(2)}) async-start(), calls=%async_computation.13 | async-start | bytes 1114112 | tf_op jit(solution)/shard_map/all_gather | solution.py:53
  176.4 694.2 %all-gather.15.cloned.1.call-start = ((), (), s32[]{:S(2)}) async-start(), calls=%async_computation.15 | async-start | bytes 1114112 | tf_op jit(solution)/shard_map/all_gather | solution.py:54
  256.8 670.9 %all-gather.17.cloned.1.call-start = ((), (), s32[]{:S(2)}) async-start(), calls=%async_computation.17 | async-start | bytes 1114112 | tf_op jit(solution)/shard_map/all_gather | solution.py:55
  337.6 667.9 %all-gather.7.cloned.1.call-start = ((), (), s32[]{:S(2)}) async-start(), calls=%async_computation.7 | async-start | bytes 4456448 | tf_op jit(solution)/shard_map/all_gather | solution.py:50
  514.5 568.5 %all-gather.9.cloned.1.call-start = ((), (), s32[]{:S(2)}) async-start(), calls=%async_computation.9 | async-start | bytes 4456448 | tf_op jit(solution)/shard_map/all_gather | solution.py:51
  1089.3 4.9 copy-start.1
  1089.3 5.9 copy-start.2
  1094.3 1.9 copy-start.3
Sparse Core Ops, SparseCore 0:
  10.3 84.1 reduce-scatter.10
  96.7 78.0 reduce-scatter.12
  177.1 78.0 reduce-scatter.14
  257.9 78.0 reduce-scatter.16
  338.2 174.2 reduce-scatter.6
  514.6 180.3 reduce-scatter.8
  698.3 57.5 all-gather.10
  759.3 53.9 all-gather.12
  816.6 53.9 all-gather.14
  873.8 53.9 all-gather.16
  931.1 74.4 all-gather.6
  1008.7 74.1 all-gather.8
where the time goes:
time: 1100 us
  waiting for transfers between devices  969 us (88%)
  blocking collectives  79.8 us (7%)
  local copies, waits for them, and re-layouts  28.4 us (3%)
  between operations  15.6 us (1%)
    reduce_scatter x1, waiting for transfers between devices, shards(): lax.psum_scatter(grad_down[0], 'batch', scatter_dimension=1, tiled=True)  180 us
    reduce_scatter x1, waiting for transfers between devices, shards(): lax.psum_scatter(grad_up[0], 'batch', scatter_dimension=0, tiled=True)  175 us
    unnamed x2, blocking collectives  79.8 us
    reduce_scatter x1, waiting for transfers between devices, shards(): lax.psum_scatter(grad_mixed[0], 'batch', scatter_dimension=1, tiled=True)  79.2 us
    reduce_scatter x1, waiting for transfers between devices, shards(): lax.psum_scatter(grad_value[0], 'batch', scatter_dimension=0, tiled=True)  78.7 us
    reduce_scatter x1, waiting for transfers between devices, shards(): lax.psum_scatter(grad_key[0], 'batch', scatter_dimension=0, tiled=True)  78.7 us
    all_gather x1, waiting for transfers between devices, shards(): lax.all_gather(new_down.astype(jnp.bfloat16), 'batch', axis=1, tiled=True)  77.4 us
    all_gather x1, waiting for transfers between devices, shards(): lax.all_gather(new_up.astype(jnp.bfloat16), 'batch', axis=0, tiled=True)  75.5 us
  transfers between devices with their start and end apart: 12, of which 11 were waited for; matrix products, arithmetic and copies ran while one was open for 2% of the time, Pallas kernels for 0%

commit v1 on v0

--- a/solution.py
+++ b/solution.py
@@ -4,6 +4,12 @@
 from jax.sharding import PartitionSpec as P
 
 learn_rate = 0.3
+
+
+def gathered_along(x, mesh_axis, d):
+    parts = lax.all_gather(x, mesh_axis, axis=0, tiled=False)
+    full = jnp.concatenate(parts, axis=d)
+    return full
 
 
 def shards(
@@ -48,7 +54,7 @@
     new_norm = weight_norm - learn_rate * mean_norm
     copy_up, copy_down, copy_query, copy_key, copy_value, copy_mixed, copy_norm = (
         lax.all_gather(new_up.astype(jnp.bfloat16), "batch", axis=0, tiled=True),
-        lax.all_gather(new_down.astype(jnp.bfloat16), "batch", axis=1, tiled=True),
+        gathered_along(new_down.astype(jnp.bfloat16), "batch", 1),
         lax.all_gather(new_query.astype(jnp.bfloat16), "batch", axis=0, tiled=True),
         lax.all_gather(new_key.astype(jnp.bfloat16), "batch", axis=0, tiled=True),
         lax.all_gather(new_value.astype(jnp.bfloat16), "batch", axis=0, tiled=True),

time: 1100 us -> 1100 us (level)
  waiting for transfers between devices: 969 us -> 954 us
    all_gather x1, waiting for transfers between devices: 75.5 us -> 62 us  [shards(): lax.all_gather(new_up.astype(jnp.bfloat16), 'batch', axis=0, tiled=True)]
    unnamed x37 -> x38, local copies, waits for them, and re-layouts: 28.4 us -> 33 us
  transfers between devices with their start and end apart: 12 -> 12, of which waited for: 11 -> 11; matrix products, arithmetic and copies ran while one was open for 2% -> 4% of each run, Pallas kernels for 0% -> 0%
where the time goes in v1:
time: 1100 us
  waiting for transfers between devices  954 us (87%)
  blocking collectives  79.8 us (7%)
  local copies, waits for them, and re-layouts  37.3 us (3%)
  between operations  15.6 us (1%)
    reduce_scatter x1, waiting for transfers between devices, shards(): lax.psum_scatter(grad_up[0], 'batch', scatter_dimension=0, tiled=True)  180 us
    reduce_scatter x1, waiting for transfers between devices, shards(): lax.psum_scatter(grad_down[0], 'batch', scatter_dimension=1, tiled=True)  175 us
    unnamed x2, blocking collectives  79.8 us
    reduce_scatter x1, waiting for transfers between devices, shards(): lax.psum_scatter(grad_mixed[0], 'batch', scatter_dimension=1, tiled=True)  79.3 us
    reduce_scatter x1, waiting for transfers between devices, shards(): lax.psum_scatter(grad_key[0], 'batch', scatter_dimension=0, tiled=True)  78.7 us
    reduce_scatter x1, waiting for transfers between devices, shards(): lax.psum_scatter(grad_value[0], 'batch', scatter_dimension=0, tiled=True)  78.4 us
    all_gather x1, waiting for transfers between devices, gathered_along(): parts = lax.all_gather(x, mesh_axis, axis=0, tiled=False)  76.2 us
    reduce_scatter x1, waiting for transfers between devices, shards(): lax.psum_scatter(grad_query[0], 'batch', scatter_dimension=0, tiled=True)  73.3 us
  transfers between devices with their start and end apart: 12, of which 11 were waited for; matrix products, arithmetic and copies ran while one was open for 4% of the time, Pallas kernels for 0%

profile of v1, /device:TPU:0, one launch (start us, length us, event | category | flops | bytes accessed | tf_op | source)
XLA Modules:
  0.0 1098.1 jit_solution(13457386707055419796)
XLA Ops:
  7.2 0.0 reduce-scatter.11.cloned.1.call-start
  7.2 0.7 reduce-scatter.11.cloned.1.call-update
  7.9 0.0 reduce-scatter.13.cloned.1.call-start
  8.0 0.7 reduce-scatter.13.cloned.1.call-update
  8.7 0.0 reduce-scatter.15.cloned.1.call-start
  8.7 0.7 reduce-scatter.15.cloned.1.call-update
  9.4 0.0 reduce-scatter.17.cloned.1.call-start
  9.5 1.8 copy.43
  11.3 0.0 reduce-scatter.9.cloned.1.call-start
  11.4 9.2 copy.41
  20.6 0.0 reduce-scatter.7.cloned.1.call-start
  20.7 0.5 reduce-scatter.7.cloned.1.call-update
  21.2 0.0 all-gather.10.cloned.1.call-start
  21.3 73.3 %reduce-scatter.11.cloned.1.call-done = f32[64,512]{1,0:T(8,128)} async-done(((f32[1024,512]{1,0:T(8,128)}), f32[64,512]{1,0:T(8,128)}) %reduce-scatter.11.cloned.1.call-update) | async-done | bytes 131088 | tf_op jit(solution)/shard_map/reduce_scatter | solution.py:34
  94.5 1.6 fusion.6
  96.2 0.0 all-gather.12.cloned.1.call-start
  96.2 78.7 %reduce-scatter.13.cloned.1.call-done = f32[64,512]{1,0:T(8,128)} async-done(((f32[1024,512]{1,0:T(8,128)}), f32[64,512]{1,0:T(8,128)}) %reduce-scatter.13.cloned.1.call-update) | async-done | bytes 131088 | tf_op jit(solution)/shard_map/reduce_scatter | solution.py:35
  174.9 1.6 fusion.5
  176.6 0.0 all-gather.14.cloned.1.call-start
  176.6 78.4 %reduce-scatter.15.cloned.1.call-done = f32[64,512]{1,0:T(8,128)} async-done(((f32[1024,512]{1,0:T(8,128)}), f32[64,512]{1,0:T(8,128)}) %reduce-scatter.15.cloned.1.call-update) | async-done | bytes 131088 | tf_op jit(solution)/shard_map/reduce_scatter | solution.py:36
  255.0 1.6 fusion.4
  256.7 0.0 all-gather.16.cloned.1.call-start
  256.7 79.3 %reduce-scatter.17.cloned.1.call-done = f32[512,64]{0,1:T(8,128)} async-done(((f32[512,1024]{0,1:T(8,128)}), f32[512,64]{0,1:T(8,128)}) %reduce-scatter.17.cloned.1.call-update) | async-done | bytes 131088 | tf_op jit(solution)/shard_map/reduce_scatter | solution.py:37
  336.0 1.6 fusion.3
  337.7 0.0 all-gather.18.cloned.1.call-start
  337.7 174.8 %reduce-scatter.9.cloned.1.call-done = f32[2048,64]{0,1:T(8,128)} async-done(((f32[2048,1024]{0,1:T(8,128)}), f32[2048,64]{0,1:T(8,128)}) %reduce-scatter.9.cloned.1.call-update) | async-done | bytes 524304 | tf_op jit(solution)/shard_map/reduce_scatter | solution.py:33
  512.5 2.0 fusion.7
  514.5 0.0 all-gather.8.cloned.1.call-start
  514.5 180.4 %reduce-scatter.7.cloned.1.call-done = f32[64,2048]{1,0:T(8,128)} async-done(((f32[1024,2048]{1,0:T(8,128)}), f32[64,2048]{1,0:T(8,128)}) %reduce-scatter.7.cloned.1.call-update) | async-done | bytes 524304 | tf_op jit(solution)/shard_map/reduce_scatter | solution.py:32
  694.9 2.0 fusion.8
  697.0 0.6 fusion.9
  698.9 42.5 %all-reduce.1 = f32[1024]{0:T(1024)S(1)} all-reduce(f32[1024]{0:T(1024)S(1)} %bitcast.25), channel_id=9, replica_groups=mesh['batch'=16,'cols'=2] {'batch'}, use_global_device_ids=true, to_apply=%region_6.0.clone | all-reduce | flops 1024 | bytes 8192
  741.4 0.6 fusion.1
  742.0 0.2 dynamic-update-slice
  742.1 37.3 %all-reduce = bf16[1024]{0:T(1024)(128)(2,1)} all-reduce(bf16[1024]{0:T(1024)(128)(2,1)S(1)} %dynamic-update-slice), channel_id=1, replica_groups=mesh['batch'=16,'cols'=2] {'batch'}, use_global_device_ids=true, to_apply=%add | all-reduce | flops 1024 | bytes 4096
  779.5 33.8 %all-gather.12.cloned.1.call-done = bf16[1024,512]{1,0:T(8,128)(2,1)} async-done(((bf16[64,512]{1,0:T(8,128)(2,1)}), bf16[1024,512]{1,0:T(8,128)(2,1)}) %all-gather.12.cloned.1.call-update) | async-done | bytes 1048592 | tf_op jit(solution)/shard_map/all_gather | solution.py:59
  813.3 57.3 %all-gather.14.cloned.1.call-done = bf16[1024,512]{1,0:T(8,128)(2,1)} async-done(((bf16[64,512]{1,0:T(8,128)(2,1)}), bf16[1024,512]{1,0:T(8,128)(2,1)}) %all-gather.14.cloned.1.call-update) | async-done | bytes 1048592 | tf_op jit(solution)/shard_map/all_gather | solution.py:60
  870.5 57.1 %all-gather.16.cloned.1.call-done = bf16[512,1024]{0,1:T(8,128)(2,1)} async-done(((bf16[512,64]{0,1:T(8,128)(2,1)}), bf16[512,1024]{0,1:T(8,128)(2,1)}) %all-gather.16.cloned.1.call-update) | async-done | bytes 1048592 | tf_op jit(solution)/shard_map/all_gather | solution.py:61
  927.7 2.3 copy.45
  929.9 76.2 %all-gather.18.cloned.1.call-done = bf16[32768,64]{0,1:T(8,128)(2,1)} async-done(((bf16[2048,64]{0,1:T(8,128)(2,1)}), bf16[32768,64]{0,1:T(8,128)(2,1)}) %all-gather.18.cloned.1.call-update) | async-done | bytes 4194320 | tf_op jit(solution)/shard_map/all_gather | solution.py:10
  1006.1 4.6 copy.46
  1010.7 4.3 copy.42
  1015.0 6.4 copy.44
  1021.4 62.0 %all-gather.8.cloned.1.call-done = bf16[1024,2048]{1,0:T(8,128)(2,1)} async-done(((bf16[64,2048]{1,0:T(8,128)(2,1)}), bf16[1024,2048]{1,0:T(8,128)(2,1)}) %all-gather.8.cloned.1.call-update) | async-done | bytes 4194320 | tf_op jit(solution)/shard_map/all_gather | solution.py:56
  1083.4 4.9 copy.52
  1088.4 1.0 copy.53
  1089.3 1.0 copy.54
  1090.3 1.0 copy.55
  (36 shorter events, 0.2 us)
Async XLA Ops:
  7.2 2.3 copy-start
  7.2 87.4 %reduce-scatter.11.cloned.1.call-start = ((), (), s32[]{:S(2)}) async-start(), calls=%async_computation.9 | async-start | bytes 2228224 | tf_op jit(solution)/shard_map/reduce_scatter | solution.py:34
  7.9 167.0 %reduce-scatter.13.cloned.1.call-start = ((), (), s32[]{:S(2)}) async-start(), calls=%async_computation.11 | async-start | bytes 2228224 | tf_op jit(solution)/shard_map/reduce_scatter | solution.py:35
  8.7 246.4 %reduce-scatter.15.cloned.1.call-start = ((), (), s32[]{:S(2)}) async-start(), calls=%async_computation.13 | async-start | bytes 2228224 | tf_op jit(solution)/shard_map/reduce_scatter | solution.py:36
  9.4 326.6 %reduce-scatter.17.cloned.1.call-start = ((), (), s32[]{:S(2)}) async-start(), calls=%async_computation.15 | async-start | bytes 2228224 | tf_op jit(solution)/shard_map/reduce_scatter | solution.py:37
  11.3 501.2 %reduce-scatter.9.cloned.1.call-start = ((), (), s32[]{:S(2)}) async-start(), calls=%async_computation.8 | async-start | bytes 8912896 | tf_op jit(solution)/shard_map/reduce_scatter | solution.py:33
  20.6 674.3 %reduce-scatter.7.cloned.1.call-start = ((), (), s32[]{:S(2)}) async-start(), calls=%async_computation.6 | async-start | bytes 8912896 | tf_op jit(solution)/shard_map/reduce_scatter | solution.py:32
  20.6 73.9 %copy-start.6 = (f32[64,512]{1,0:T(8,128)S(1)}, f32[64,512]{1,0:T(8,128)}, u32[]{:S(2)}) copy-start(f32[64,512]{1,0:T(8,128)} %param.23) | copy-start | bytes 393220
  20.7 154.3 %copy-start.7 = (f32[64,512]{1,0:T(8,128)S(1)}, f32[64,512]{1,0:T(8,128)}, u32[]{:S(2)}) copy-start(f32[64,512]{1,0:T(8,128)} %param.24) | copy-start | bytes 393220
  20.7 234.4 %copy-start.8 = (f32[64,512]{1,0:T(8,128)S(1)}, f32[64,512]{1,0:T(8,128)}, u32[]{:S(2)}) copy-start(f32[64,512]{1,0:T(8,128)} %param.25) | copy-start | bytes 393220
  20.7 315.4 %copy-start.9 = (f32[512,64]{0,1:T(8,128)S(1)}, f32[512,64]{0,1:T(8,128)}, u32[]{:S(2)}) copy-start(f32[512,64]{0,1:T(8,128)} %param.26) | copy-start | bytes 393220
  20.7 491.8 %copy-start.4 = (f32[2048,64]{0,1:T(8,128)S(1)}, f32[2048,64]{0,1:T(8,128)}, u32[]{:S(2)}) copy-start(f32[2048,64]{0,1:T(8,128)} %param.22) | copy-start | bytes 1572868
  21.2 673.8 %copy-start.5 = (f32[64,2048]{1,0:T(8,128)S(1)}, f32[64,2048]{1,0:T(8,128)}, u32[]{:S(2)}) copy-start(f32[64,2048]{1,0:T(8,128)} %param.21) | copy-start | bytes 1572868
  21.2 675.8 %copy-start.11 = (u32[32]{0:T(128)S(1)}, u32[32]{0:T(128)}, u32[]{:S(2)}) copy-start(u32[32]{0:T(128)} %constant.27) | copy-start | bytes 388
  21.2 677.6 %copy-start.10 = (f32[1,1024]{1,0:T(1,128)S(1)}, f32[1,1024]{1,0:T(1,128)}, u32[]{:S(2)}) copy-start(f32[1,1024]{1,0:T(1,128)} %param.20) | copy-start | bytes 12292
  21.2 720.2 %copy-start.12 = (f32[64]{0:T(128)S(1)}, f32[64]{0:T(128)}, u32[]{:S(2)}) copy-start(f32[64]{0:T(128)} %param.27) | copy-start | bytes 772
  21.2 758.2 %all-gather.10.cloned.1.call-start = ((), (), s32[]{:S(2)}) async-start(), calls=%async_computation.10 | async-start | bytes 1114112 | tf_op jit(solution)/shard_map/all_gather | solution.py:58
  96.2 717.1 %all-gather.12.cloned.1.call-start = ((), (), s32[]{:S(2)}) async-start(), calls=%async_computation.12 | async-start | bytes 1114112 | tf_op jit(solution)/shard_map/all_gather | solution.py:59
  176.6 694.0 %all-gather.14.cloned.1.call-start = ((), (), s32[]{:S(2)}) async-start(), calls=%async_computation.14 | async-start | bytes 1114112 | tf_op jit(solution)/shard_map/all_gather | solution.py:60
  256.7 671.0 %all-gather.16.cloned.1.call-start = ((), (), s32[]{:S(2)}) async-start(), calls=%async_computation.16 | async-start | bytes 1114112 | tf_op jit(solution)/shard_map/all_gather | solution.py:61
  337.7 668.4 %all-gather.18.cloned.1.call-start = ((), (), s32[]{:S(2)}) async-start(), calls=%async_computation.17 | async-start | bytes 4456448 | tf_op jit(solution)/shard_map/all_gather | solution.py:10
  514.5 568.9 %all-gather.8.cloned.1.call-start = ((), (), s32[]{:S(2)}) async-start(), calls=%async_computation.7 | async-start | bytes 4456448 | tf_op jit(solution)/shard_map/all_gather | solution.py:56
  1083.4 4.9 copy-start.1
  1083.4 5.9 copy-start.2
  1088.4 1.9 copy-start.3
Sparse Core Ops, SparseCore 0:
  10.3 84.2 reduce-scatter.10
  96.8 78.0 reduce-scatter.12
  177.2 77.7 reduce-scatter.14
  257.7 78.2 reduce-scatter.16
  338.2 174.2 reduce-scatter.8
  514.6 180.2 reduce-scatter.6
  698.3 57.6 all-gather.9
  759.2 53.9 all-gather.11
  816.6 53.9 all-gather.13
  873.7 53.9 all-gather.15
  931.0 75.0 all-gather.17
  1009.3 74.0 all-gather.7
